TPU v7x, 256 devices: a 2x2x32 block of a 4x8x32 slice. The times are simulated.
256 devices in a mesh: groups: 4 (over y, x), blk: 32 (over z), sub: 2 (over core).
Axes of the slice: x: 2, y: 2, z: 32, core: 2. Of those that a mesh axis runs over, the one named last changes fastest.
The devices are a block of a 4x8x32 slice.
Arguments:
- embeddings: bfloat16 [49152, 1024], P(('groups', 'blk', 'sub')), parts along dimension 0, may hold values from -6 to 6
- member_key: int32 [49152], P(('groups', 'blk', 'sub')), parts along dimension 0, may hold values from 0 to 1073741823, as said below
- limit_index: int32 [4], P('groups'), parts along dimension 0, may hold values from 0 to 7
Outputs:
- max_cosine: float32 [49152], P(('groups', 'blk', 'sub')), parts along dimension 0
- kept_share: float32 [4], P('groups'), parts along dimension 0
There are 4 independent parts, one for each index of `groups`. A program takes and returns all parts, laid end to end along the dimension named above; each array names one. Nothing has to cross between parts.
Inputs may be any that keep to these rules, and one draw needn't show every extreme that they name: `member_key`: all keys of a cluster are distinct. A key's quotient by 268435456 is the member's sub-cluster, 0 to 3; its remainder orders the members.
All inputs are finite; a program needn't handle non-finite values.
Results may differ from a plain program's by a relative error of at most 0.0013.
Values may be sent and summed in bfloat16 or wider, within the bound.
No kernel may reach another device: no remote copies, remote signals or barrier semaphores. Data moves between devices by JAX's collectives and lax.ppermute only.
A program may use at most 64 MiB of HBM per device.

v0:
```python
import math
import jax
import jax.numpy as jnp
from jax import lax
from jax.sharding import PartitionSpec as P

LIMITS = 8
label_stride = 268435456


def joined_along(pieces, dim):
    dims = list(pieces.shape[1:])
    dims[dim] *= pieces.shape[0]
    return jnp.moveaxis(pieces, 0, dim).reshape(dims)


def all_blocks(shard, axes, turns):
    pieces = shard
    for k in turns:
        pieces = lax.all_gather(pieces, axes[k])
    done = turns[::-1]
    back = [done.index(k) for k in range(len(axes))]
    pieces = pieces.transpose(*back, *range(len(axes), pieces.ndim))
    return pieces.reshape(-1, *shard.shape)


def whole_of(shard, axes, turns, dim):
    return joined_along(all_blocks(shard, axes, turns), dim)


def from_everyone(shard, axis):
    devices = lax.axis_size(axis)
    return lax.all_to_all(
        jnp.broadcast_to(shard[None], (devices, *shard.shape)), axis, 0, 0, tiled=True
    )


def taken_together(shard, axis):
    return from_everyone(shard, axis).sum(axis=0)


def normalize(embeddings):
    values = embeddings.astype(jnp.float32)
    mean_square = jnp.mean(values * values, axis=1, keepdims=True)
    scaled = values * lax.rsqrt(mean_square + 1e-06) * (1.0 / math.sqrt(values.shape[1]))
    return scaled.astype(jnp.bfloat16)


def make_absorb(rows, row_key, key_seen):
    row_label = row_key // label_stride

    def absorb(best, piece, start):
        other_label = key_seen // label_stride
        scores = lax.dot_general(
            rows, piece, (((1,), (1,)), ((), ())), preferred_element_type=jnp.float32
        )
        allowed = (key_seen[None, :] < row_key[:, None]) & (
            other_label[None, :] == row_label[:, None]
        )
        return jnp.maximum(best, jnp.max(jnp.where(allowed, scores, jnp.float32(-1.0)), axis=1))

    return absorb


def on_device(embeddings, member_key, limit_index):
    unit = normalize(embeddings)
    own_rows = unit.shape[0]
    key_all = whole_of(member_key, ("blk", "sub"), (0, 1), 0)
    chip_unit = lax.all_gather(unit, "sub", axis=0, tiled=True)
    core = lax.axis_index("sub")
    begin = lax.axis_index("blk") * (2 * own_rows)
    chip_key = lax.dynamic_slice_in_dim(key_all, begin, 2 * own_rows, 0)
    half_key = lax.dynamic_index_in_dim(
        key_all.reshape(-1, 2, own_rows), core, 1, keepdims=False
    ).reshape(-1)
    absorb = make_absorb(chip_unit, chip_key, half_key)
    start_best = jnp.full((2 * own_rows,), -1.0, jnp.float32)
    half_best = absorb(start_best, lax.all_gather(unit, "blk", axis=0, tiled=True), jnp.int32(0))
    chip_best = lax.pmax(half_best, "sub")
    max_cosine = lax.dynamic_slice_in_dim(chip_best, core * own_rows, own_rows, 0)
    width = math.sqrt(unit.shape[1])
    table = (2.0 + 0.5 * jnp.arange(LIMITS, dtype=jnp.float32)) / width
    limit = jnp.sum(
        jnp.where(jnp.arange(LIMITS, dtype=jnp.int32) == limit_index[0], table, jnp.float32(0.0))
    )
    kept = jax.nn.sigmoid(2.0 * width * (limit - max_cosine))
    kept_sum = taken_together(jnp.sum(kept), ("blk", "sub"))
    kept_share = (kept_sum / key_all.shape[0]).reshape(1)
    return (max_cosine, kept_share)


def solution(mesh):
    in_specs = (P(("groups", "blk", "sub"), None), P(("groups", "blk", "sub")), P("groups"))
    out_specs = (P(("groups", "blk", "sub")), P("groups"))
    return jax.shard_map(
        on_device, mesh=mesh, in_specs=in_specs, out_specs=out_specs, check_vma=False
    )
```

profile of v0, /device:TPU:37, one launch (start us, length us, event | category | flops | bytes accessed | tf_op | source)
XLA Modules:
  0.0 249.5 jit_solution(8639615771263818158)
XLA Ops:
  7.2 0.1 all-gather.4.cloned.1.call-start
  7.2 1.2 fusion
  8.4 1.9 fusion.2
  10.3 0.1 all-gather.4.cloned.1.call-update
  11.1 1.3 dynamic-slice.4
  13.0 0.9 dynamic-update-slice
  13.9 112.4 %all-reduce = s32[6144]{0:T(1024)S(1)} all-reduce(s32[6144]{0:T(1024)S(1)} %dynamic-update-slice), channel_id=2, replica_groups=mesh['groups'=4,'blk'=32,'sub'=2] {'blk'}, use_global_device_ids=true, to_apply=%add | all-reduce | flops 6144 | bytes 49152
  126.2 0.1 reshape.56
  126.3 19.7 %all-gather.1 = s32[64,192]{1,0:T(8,128)S(1)} all-gather(s32[32,192]{1,0:T(8,128)S(1)} %reshape.56), channel_id=3, replica_groups=mesh['groups'=4,'blk'=32,'sub'=2] {'sub'}, dimensions={0}, use_global_device_ids=true | all-gather | bytes 73728 | tf_op jit(solution)/shard_map/all_gather | solution.py:20
  146.1 0.1 lt.26
  146.2 0.1 copy.7
  146.2 0.1 reshape_reshape.3
  146.3 0.7 fusion.8
  147.0 0.1 add_select_fusion.1
  147.1 2.6 %all_gather.22 = bf16[384,1024]{1,0:T(8,128)(2,1)S(1)} all-gather(bf16[192,1024]{1,0:T(8,128)(2,1)} %fusion.2), channel_id=1, replica_groups=mesh['groups'=4,'blk'=32,'sub'=2] {'sub'}, dimensions={0}, use_global_device_ids=true | all-gather | bytes 1179648 | tf_op jit(solution)/shard_map/all_gather | solution.py:69
  149.7 31.2 %all-gather.4.cloned.1.call-done = bf16[6144,1024]{1,0:T(8,128)(2,1)} async-done(((bf16[192,1024]{1,0:T(8,128)(2,1)}), bf16[6144,1024]{1,0:T(8,128)(2,1)}) %all-gather.4.cloned.1.call-update) | async-done | bytes 12582928 | tf_op jit(solution)/shard_map/all_gather | solution.py:78
  180.9 8.7 %select_reduce_fusion = f32[384]{0:T(512)S(1)} fusion(bf16[384,1024]{1,0:T(8,128)(2,1)S(1)} %all_gather.22, bf16[6144,1024]{1,0:T(8,128)(2,1)} %all-gather.4.cloned.1.call-done, s32[6144]{0:T(1024)S(1)} %add_select_fusion, s32[6144]{0:T(1024)S(1)} %lt.26, s32[384]{0:T(512)S(1)} %get-tuple-element.4, s32[384]{0:T(512)S(1)} %get-tuple-element.5), kind=kOutput, calls=%fused_computation | convolution fusion | flops 4843634176 | bytes 13423104 | tf_op jit(solution)/shard_map/dot_general | solution.py:54
  189.6 10.0 %pmax.7 = f32[384]{0:T(512)S(1)} all-reduce(f32[384]{0:T(512)S(1)} %broadcast_maximum_fusion), channel_id=1, replica_groups=mesh['groups'=4,'blk'=32,'sub'=2] {'sub'}, use_global_device_ids=true, to_apply=%region_2.3 | all-reduce | flops 384 | bytes 3072 | tf_op jit(solution)/shard_map/pmax | solution.py:79
  199.7 1.9 fusion.7
  201.6 0.7 broadcast_in_dim.24
  202.2 38.0 %all_to_all.6 = f32[64,1,1]{2,1,0:T(1,128)S(1)} all-to-all(f32[64,1,1]{2,1,0:T(1,128)S(1)} %broadcast_in_dim.24), channel_id=1, replica_groups=mesh['groups'=4,'blk'=32,'sub'=2] {'blk','sub'}, dimensions={0} | all-to-all | bytes 512 | tf_op jit(solution)/shard_map/all_to_all | solution.py:33
  240.2 0.7 reduce_sum.39
  (5 shorter events, 0.0 us)
Async XLA Ops:
  7.2 173.7 %all-gather.4.cloned.1.call-start = ((), (), s32[]{:S(2)}) async-start(), calls=%async_computation.1 | async-start | bytes 12976128 | tf_op jit(solution)/shard_map/all_gather | solution.py:78
Sparse Core Ops, SparseCore 0:
  10.5 170.3 all-gather.3
where the time goes:
time: 250 us
  blocking collectives  183 us (73%)
  waiting for transfers between devices  31.3 us (13%)
  between operations  17.2 us (7%)
  matrix products  8.69 us (3%)
  other arithmetic  6.44 us (3%)
  local copies, waits for them, and re-layouts  3.14 us (1%)
    unnamed x1, blocking collectives  112 us
    all_to_all x1, blocking collectives, from_everyone(): lax.all_to_all(jnp.broadcast_to(shard[None], (devices, *shard.shape)), ax...  38 us
    all_gather x1, waiting for transfers between devices, on_device(): lax.all_gather(unit, 'blk', axis=0, tiled=True)  31.2 us
    all_gather x1, blocking collectives, all_blocks(): pieces = lax.all_gather(pieces, axes[k])  19.7 us
    pmax x1, blocking collectives, on_device(): chip_best = lax.pmax(half_best, 'sub')  10 us
    dot_general x1, matrix products, absorb(): lax.dot_general(rows, piece, (((1,), (1,)), ((), ())), preferred_element_...  8.69 us
  transfers between devices with their start and end apart: 1, of which 1 were waited for; matrix products, arithmetic and copies ran while one was open for 1% of the time, Pallas kernels for 0%

commit v1 on v0

--- a/solution.py
+++ b/solution.py
@@ -3,9 +3,16 @@
 import jax.numpy as jnp
 from jax import lax
 from jax.sharding import PartitionSpec as P
+from jax.lax import all_to_all, axis_size
 
 LIMITS = 8
 label_stride = 268435456
+
+
+def treat_screen(named_axis, field):
+    n_dev_all = axis_size(named_axis)
+    tile_out = jnp.tile(field, [n_dev_all if s == 0 else 1 for s in range(field.ndim)])
+    return all_to_all(tile_out, named_axis, split_axis=0, concat_axis=0, tiled=True)
 
 
 def joined_along(pieces, dim):
@@ -75,7 +82,7 @@
     ).reshape(-1)
     absorb = make_absorb(chip_unit, chip_key, half_key)
     start_best = jnp.full((2 * own_rows,), -1.0, jnp.float32)
-    half_best = absorb(start_best, lax.all_gather(unit, "blk", axis=0, tiled=True), jnp.int32(0))
+    half_best = absorb(start_best, treat_screen("blk", unit), jnp.int32(0))
     chip_best = lax.pmax(half_best, "sub")
     max_cosine = lax.dynamic_slice_in_dim(chip_best, core * own_rows, own_rows, 0)
     width = math.sqrt(unit.shape[1])

time: 250 us -> 1290 us (5.16)
  blocking collectives: 183 us -> 1230 us
  starting transfers between devices: 0.06 us -> 33.3 us
  waiting for transfers between devices: 31.3 us -> 0.01 us
  between operations: 17.2 us -> 3.8 us
    unnamed x1, blocking collectives: 112 us -> 1160 us
    all_to_all x0 -> x1, starting transfers between devices: none -> 33.3 us  [treat_screen(): all_to_all(tile_out, named_axis, split_axis=0, concat_axis=0, tiled=True)]
    all_gather x1 -> x0, waiting for transfers between devices: 31.2 us -> none  [on_device(): lax.all_gather(unit, 'blk', axis=0, tiled=True)]
  transfers between devices with their start and end apart: 1 -> 1, of which waited for: 1 -> 0; matrix products, arithmetic and copies ran while one was open for 1% -> 0% of each run, Pallas kernels for 0% -> 0%
where the time goes in v1:
time: 1290 us
  blocking collectives  1230 us (95%)
  starting transfers between devices  33.3 us (3%)
    unnamed x1, blocking collectives  1160 us
    all_to_all x1, blocking collectives, from_everyone(): lax.all_to_all(jnp.broadcast_to(shard[None], (devices, *shard.shape)), ax...  41 us
    all_to_all x1, starting transfers between devices, treat_screen(): all_to_all(tile_out, named_axis, split_axis=0, concat_axis=0, tiled=True)  33.3 us
    all_gather x1, blocking collectives, all_blocks(): pieces = lax.all_gather(pieces, axes[k])  26.7 us
  transfers between devices with their start and end apart: 1, of which 0 were waited for; matrix products, arithmetic and copies ran while one was open for 0% of the time, Pallas kernels for 0%

profile of v1, /device:TPU:37, one launch (start us, length us, event | category | flops | bytes accessed | tf_op | source)
XLA Modules:
  0.0 1288.5 jit_solution(4841362693350113522)
XLA Ops:
  0.6 1.2 fusion
  1.8 1.2 fusion.2
  3.0 6.1 tile.2
  9.0 0.0 copy-start.1
  9.0 0.0 copy-start
  9.0 33.3 %all-to-all-start = ((bf16[32,192,1024]{2,1,0:T(8,128)(2,1)}), bf16[32,192,1024]{2,1,0:T(8,128)(2,1)}, u32[]{:S(2)}, u32[]{:S(2)}) async-start(bf16[32,192,1024]{2,1,0:T(8,128)(2,1)} %tile.2), calls=%async_computation | async-start | bytes 25165824 | tf_op jit(solution)/shard_map/all_to_all | solution.py:15
  42.4 0.0 copy-done.1
  42.4 0.6 dynamic-slice.4
  43.7 0.0 copy-done
  43.7 0.3 dynamic-update-slice
  44.0 1156.5 %all-reduce = s32[6144]{0:T(1024)S(1)} all-reduce(s32[6144]{0:T(1024)S(1)} %dynamic-update-slice), channel_id=2, replica_groups=mesh['groups'=4,'blk'=32,'sub'=2] {'blk'}, use_global_device_ids=true, to_apply=%add | all-reduce | flops 6144 | bytes 49152
  1200.5 0.1 reshape.63
  1200.6 26.7 %all-gather.1 = s32[64,192]{1,0:T(8,128)S(1)} all-gather(s32[32,192]{1,0:T(8,128)S(1)} %reshape.63), channel_id=3, replica_groups=mesh['groups'=4,'blk'=32,'sub'=2] {'sub'}, dimensions={0}, use_global_device_ids=true | all-gather | bytes 73728 | tf_op jit(solution)/shard_map/all_gather | solution.py:27
  1227.3 0.1 lt.26
  1227.4 0.1 copy.7
  1227.4 0.1 reshape_reshape.3
  1228.2 0.6 fusion.8
  1228.8 0.1 add_select_fusion.1
  1228.9 2.4 all_gather.19
  1231.3 0.0 all-to-all-done
  1231.3 8.7 select_reduce_fusion
  1240.0 2.5 pmax.7
  1242.6 1.9 fusion.7
  1244.4 0.7 broadcast_in_dim.24
  1245.1 41.0 %all_to_all.15 = f32[64,1,1]{2,1,0:T(1,128)S(1)} all-to-all(f32[64,1,1]{2,1,0:T(1,128)S(1)} %broadcast_in_dim.24), channel_id=1, replica_groups=mesh['groups'=4,'blk'=32,'sub'=2] {'blk','sub'}, dimensions={0} | all-to-all | bytes 512 | tf_op jit(solution)/shard_map/all_to_all | solution.py:40
  1286.1 0.7 reduce_sum.39
  (5 shorter events, 0.0 us)
Async XLA Ops:
  9.0 33.4 %copy-start.1 = (u32[256]{0:T(256)S(1)}, u32[256]{0:T(256)}, u32[]{:S(2)}) copy-start(u32[256]{0:T(256)} %constant.77) | copy-start | bytes 3076
  9.0 34.6 %copy-start = (s32[192]{0:T(256)S(1)}, s32[192]{0:T(256)}, u32[]{:S(2)}) copy-start(s32[192]{0:T(256)} %param.4) | copy-start | bytes 2308
  9.0 1222.3 %all-to-all-start = ((bf16[32,192,1024]{2,1,0:T(8,128)(2,1)}), bf16[32,192,1024]{2,1,0:T(8,128)(2,1)}, u32[]{:S(2)}, u32[]{:S(2)}) async-start(bf16[32,192,1024]{2,1,0:T(8,128)(2,1)} %tile.2), calls=%async_computation | async-start | bytes 25165824 | tf_op jit(solution)/shard_map/all_to_all | solution.py:15
